TPU v7x, 8 devices: a whole 2x2x1 slice. The times are simulated.
8 devices in a mesh: col: 2 (over z, y), row: 2 (over x), depth: 2 (over core).
Axes of the slice: x: 2, y: 2, z: 1, core: 2. Of those that a mesh axis runs over, the one named last changes fastest.
Arguments:
- a_mat: bfloat16 [8192, 16384], P(('depth', 'row', 'col'))
- b_mat: bfloat16 [16384, 10240], P(('depth', 'row', 'col'))
Outputs:
- output: bfloat16 [8192, 10240], P(('depth', 'row', 'col'))
All inputs are finite; a program needn't handle non-finite values.
Results may differ from a plain program's by a relative error of at most 0.001.
Values are sent between devices in bfloat16 or wider.
A program may use at most 1 GiB of HBM per device.

v0:
```python
import functools

import jax
import jax.numpy as jnp
from jax import lax
from jax.experimental import pallas as pl
from jax.experimental.pallas import tpu as pltpu
from jax.sharding import PartitionSpec as P


MESH = pl.DeviceIdType.MESH
BLOCK = 512
TILES = 4
AHEAD = 4
SLOTS = 3
PARTS = (28, 3, 1)
HUB = (1, 0)
SLAB = (16, 3)
ROUND = 8
PIECES = 1
RING = 2 * (SLOTS + 1)


def kernel(
    n_blocks, tile, a_ref, b_ref, c_ref, r_got, q_done, b_got, relay, *others,
):
    p_parts, q_parts, scratch = others[: len(PARTS)], others[len(PARTS) : 2 * len(PARTS)], others[2 * len(PARTS) :]
    (
        a_buf, b_buf, p_buf, q_buf, r_buf, c_buf,
        a_own_sem, a_send, a_recv, b_send, b_recv, b_load_sem, first_send, first_recv, p_send, r_recv,
        r_load_sem, c_sem, q_sem, last_sem, here_sem, hop_send, hop_recv,
    ) = scratch
    last = n_blocks - 1
    col, row, core = lax.axis_index("col"), lax.axis_index("row"), lax.axis_index("depth")
    neighbour, partner, sibling = {"col": 1 - col}, {"row": 1 - row}, {"depth": 1 - core}
    depth, block = b_ref.shape[0], b_buf.shape[2]

    def rows_of(m):
        return pl.ds(pl.multiple_of(m * tile, tile), tile)

    def cols_of(t):
        return pl.ds(pl.multiple_of(t * block, block), block)

    def a_cols(h, r):
        return pl.ds(pl.multiple_of((h * 4 + r * 2) * depth, depth), 2 * depth)

    def a_half(h):
        return pl.ds(h * 2 * depth, 2 * depth)

    def own_a(h):
        return pltpu.make_async_copy(a_ref.at[:, a_cols(h, row)], a_buf.at[0, :, a_half(h)], a_own_sem.at[h])

    def send_a(m, h):
        return pltpu.make_async_remote_copy(
            src_ref=a_ref.at[rows_of(m), a_cols(h, 1 - row)], dst_ref=a_buf.at[1, rows_of(m), a_half(h)],
            send_sem=a_send.at[m, h], recv_sem=a_recv.at[m, h], device_id=partner, device_id_type=MESH)

    def send_b(way, t):
        return pltpu.make_async_remote_copy(
            src_ref=b_got.at[0, t] if way == 2 else b_ref.at[:, cols_of(t)], dst_ref=b_got.at[way, t],
            send_sem=b_send.at[way, lax.rem(t, RING)], recv_sem=b_recv.at[way, lax.rem(t, RING)],
            device_id=neighbour if way == 0 else sibling, device_id_type=MESH)

    def load_b(t, slot):
        places = (core * 2 + col, core * 2 + 1 - col, (1 - core) * 2 + col, (1 - core) * 2 + 1 - col)
        return [
            pltpu.make_async_copy(
                b_ref.at[:, cols_of(t)] if i == 0 else b_got.at[i - 1, t],
                b_buf.at[slot, pl.ds(pl.multiple_of(place * depth, depth), depth), :], b_load_sem.at[slot, i])
            for i, place in enumerate(places)
        ]

    def send_first(m):
        return pltpu.make_async_remote_copy(
            src_ref=p_buf.at[0, rows_of(m)], dst_ref=r_got.at[0, rows_of(m)],
            send_sem=first_send.at[m], recv_sem=first_recv.at[m], device_id=partner, device_id_type=MESH)

    def send_block(s):
        return pltpu.make_async_remote_copy(
            src_ref=p_buf.at[lax.rem(s, SLOTS)], dst_ref=r_got.at[s],
            send_sem=p_send.at[lax.rem(s, SLOTS)], recv_sem=r_recv.at[lax.rem(s, RING)], device_id=partner, device_id_type=MESH)

    slab, rest = pl.ds(0, SLAB[0]), pl.ds(SLAB[0], p_buf.shape[1] - SLAB[0])
    wide = SLAB[1] * block // 4
    side, corner = pl.ds(0, wide), pl.ds(wide, block - wide)

    def at(c, r):
        return jnp.logical_and(core == 1, jnp.logical_and(col == c, row == r))

    def send_rest():
        return [
            pltpu.make_async_remote_copy(
                src_ref=p_buf.at[ROUND % SLOTS, *part], dst_ref=r_got.at[ROUND, *part],
                send_sem=send, recv_sem=recv, device_id=partner, device_id_type=MESH)
            for part, send, recv in (
                ((rest, slice(None)), p_send.at[ROUND % SLOTS], r_recv.at[ROUND % RING]),
                ((slab, corner), hop_send.at[3], hop_recv.at[3]),
            )
        ]

    def hop(i):
        sources = (p_buf.at[ROUND % SLOTS, slab, side], relay.at[0], relay.at[1])
        targets = (relay.at[0], relay.at[1], r_got.at[ROUND, slab, side])
        return pltpu.make_async_remote_copy(
            src_ref=sources[i], dst_ref=targets[i], send_sem=hop_send.at[i], recv_sem=hop_recv.at[i],
            device_id=partner if i == 1 else neighbour, device_id_type=MESH)

    def load_r(q):
        return pltpu.make_async_copy(r_got.at[q], r_buf, r_load_sem)

    def store_c(q):
        return pltpu.make_async_copy(c_buf, c_ref.at[:, cols_of(q)], c_sem)

    unit = p_buf.shape[1] // sum(PARTS)
    parts = [pl.ds(sum(PARTS[:i]) * unit, n * unit) for i, n in enumerate(PARTS)]

    def store_q_done():
        return pltpu.make_async_copy(q_buf, q_done, q_sem.at[0])

    def store_q():
        return [
            pltpu.make_async_copy(q_buf.at[part], out, q_sem.at[i])
            for i, (part, out) in enumerate(zip(parts, q_parts))
        ]

    def store_p():
        return [
            pltpu.make_async_copy(p_buf.at[last % SLOTS, part], out, last_sem.at[i])
            for i, (part, out) in enumerate(zip(parts, p_parts))
        ]

    def product(whose, m, slot):
        return jnp.dot(a_buf[whose, rows_of(m), :], b_buf[slot], preferred_element_type=jnp.float32)

    def pass_on(t):
        @pl.when(t >= RING - AHEAD)
        def _():
            send_b(0, t + AHEAD - RING).wait_send()

        @pl.when(t >= RING)
        def _():
            send_b(1, t - RING).wait_send()
            send_b(2, t - RING).wait_send()

        send_b(0, t).wait_recv()
        send_b(2, t).start()
        send_b(1, t).start()

        @pl.when(t + AHEAD < n_blocks)
        def _():
            send_b(0, t + AHEAD).start()

    def start_load_first(t):
        send_b(1, t).wait_recv()
        send_b(2, t).wait_recv()
        for copy in load_b(t, 0):
            copy.start()

    barrier = pltpu.get_barrier_semaphore()
    is_hub = jnp.logical_and(col == HUB[0], core == HUB[1])
    pl.semaphore_signal(barrier, inc=1, device_id=partner, device_id_type=MESH)

    @pl.when(jnp.logical_not(is_hub))
    def _():
        hub = {"col": HUB[0], "depth": HUB[1]}
        pl.semaphore_signal(barrier, inc=1, device_id=hub, device_id_type=MESH)
        pl.semaphore_wait(barrier, 1)

    @pl.when(is_hub)
    def _():
        pl.semaphore_wait(barrier, 4)
        for other in (neighbour, sibling, {**neighbour, **sibling}):
            pl.semaphore_signal(here_sem, inc=1, device_id=other, device_id_type=MESH)

    def start_a(tiles):
        for m in tiles:
            for h in range(2):
                send_a(m, h).start()

    early, late = range(2), range(2, TILES)
    start_a(early)

    @pl.when(jnp.logical_not(is_hub))
    def _():
        pl.semaphore_wait(here_sem, 1)

    for t in range(AHEAD):
        send_b(0, t).start()

    @pl.when(core == 0)
    def _():
        start_a(late)

    for h in range(2):
        own_a(h).start()
    pass_on(0)
    pass_on(1)
    start_load_first(0)

    @pl.loop(2, AHEAD)
    def _(t):
        pass_on(t)

    for h in range(2):
        own_a(h).wait()
    for copy in load_b(0, 0):
        copy.wait()

    @pl.loop(0, n_blocks + SLOTS)
    def _(s):
        @pl.when(s < n_blocks)
        def _():
            @pl.when(s > 0)
            def _():
                for copy in load_b(s, 0):
                    copy.wait()

            @pl.when(s == SLOTS)
            def _():
                for m in range(TILES):
                    send_first(m).wait_send()

            slab_sent = jnp.logical_and(s == ROUND + SLOTS, at(0, 1))

            @pl.when(jnp.logical_and(s > SLOTS, jnp.logical_not(slab_sent)))
            def _():
                send_block(s - SLOTS).wait_send()

            @pl.when(slab_sent)
            def _():
                for copy in (*send_rest(), hop(0)):
                    copy.wait_send()

            @pl.loop(0, TILES)
            def _(m):
                @pl.when(s == 0)
                def _():
                    for h in range(2):
                        send_a(m, h).wait_recv()

                p_buf[lax.rem(s, SLOTS), rows_of(m), :] = product(1, m, 0)

                held = jnp.logical_and(core == 1, m < len(early))

                @pl.when(jnp.logical_and(s == 0, jnp.logical_not(held)))
                def _():
                    send_first(m).start()

                @pl.when(jnp.logical_and(jnp.logical_and(s == 0, core == 1), m == len(early) - 1))
                def _():
                    start_a(late)
                    for first in early:
                        send_first(first).start()

            @pl.when(s == last)
            def _():
                for copy in store_p():
                    copy.start()

            slab_goes = jnp.logical_and(s == ROUND, at(0, 1))

            @pl.when(jnp.logical_and(jnp.logical_and(s > 0, s < last), jnp.logical_not(slab_goes)))
            def _():
                send_block(s).start()

            @pl.when(slab_goes)
            def _():
                for copy in (*send_rest(), hop(0)):
                    copy.start()

            for i, place in ((1, (1, 1)), (2, (1, 0))):
                @pl.when(jnp.logical_and(s == ROUND + i, at(*place)))
                def _():
                    hop(i - 1).wait_recv()
                    hop(i).start()

            @pl.when(s + AHEAD < n_blocks)
            def _():
                pass_on(s + AHEAD)

            @pl.when(s + 1 < n_blocks)
            def _():
                start_load_first(s + 1)

        @pl.when(s >= SLOTS)
        def _():
            q = s - SLOTS

            @pl.when(q == 0)
            def _():
                for m in range(TILES):
                    send_first(m).wait_recv()

            slab_comes = jnp.logical_and(q == ROUND, at(0, 0))

            @pl.when(jnp.logical_and(jnp.logical_and(q > 0, q < last - 1), jnp.logical_not(slab_comes)))
            def _():
                send_block(q).wait_recv()

            @pl.when(slab_comes)
            def _():
                for copy in (*send_rest(), hop(2)):
                    copy.wait_recv()

            @pl.when(q < last - 1)
            def _():
                load_r(q).start()

            for copy in load_b(q, 1):
                copy.wait()

            @pl.when(q == last)
            def _():
                store_q_done().wait()

            @pl.loop(0, TILES)
            def _(m):
                q_buf[rows_of(m), :] = product(0, m, 1)

            @pl.when(q == last - 1)
            def _():
                store_q_done().start()

            @pl.when(q == last)
            def _():
                for copy in store_q():
                    copy.start()

            @pl.when(q + 1 < n_blocks)
            def _():
                for copy in load_b(q + 1, 1):
                    copy.start()

            @pl.when(q < last - 1)
            def _():
                load_r(q).wait()

                @pl.when(q > 0)
                def _():
                    store_c(q - 1).wait()

                @pl.loop(0, TILES)
                def _(m):
                    rows = rows_of(m)
                    c_buf[rows, :] = (q_buf[rows, :] + r_buf[rows, :]).astype(c_buf.dtype)

                store_c(q).start()

        @pl.when(s == SLOTS - 1)
        def _():
            for copy in load_b(0, 1):
                copy.start()

    @pl.loop(n_blocks - RING, n_blocks)
    def _(t):
        send_b(1, t).wait_send()
        send_b(2, t).wait_send()

        @pl.when(t >= n_blocks - RING + AHEAD)
        def _():
            send_b(0, t).wait_send()

    for i, place in ((1, (1, 1)), (2, (1, 0))):
        @pl.when(at(*place))
        def _():
            hop(i).wait_send()

    store_c(last - 2).wait()
    for copy in store_q() + store_p():
        copy.wait()
    for m in range(TILES):
        for h in range(2):
            send_a(m, h).wait_send()

    @pl.loop(n_blocks - SLOTS, last)
    def _(s):
        send_block(s).wait_send()

    send_block(last - 1).wait_recv()


def write_out(c_ref, q_ref, r_ref, out_ref, c_buf, q_buf, r_buf, o_buf, load_sem, store_sem):
    rows, done = c_buf.shape
    step = rows // PIECES

    def load(i):
        some = pl.ds(i * step, step)
        return pltpu.make_async_copy(c_ref.at[some, pl.ds(0, done)], c_buf.at[some], load_sem.at[i])

    def store(i):
        some = pl.ds(i * step, step)
        return pltpu.make_async_copy(c_buf.at[some], out_ref.at[some, pl.ds(0, done)], store_sem.at[i])

    load_q = pltpu.make_async_copy(q_ref, q_buf, load_sem.at[PIECES])
    load_r = pltpu.make_async_copy(r_ref.at[r_ref.shape[0] - 1], r_buf, load_sem.at[PIECES + 1])
    store_sum = pltpu.make_async_copy(o_buf, out_ref.at[:, pl.ds(done, o_buf.shape[1])], store_sem.at[PIECES])
    load_q.start()
    load_r.start()
    for i in range(PIECES):
        load(i).start()
    for i in range(PIECES):
        load(i).wait()
        store(i).start()
    load_q.wait()
    load_r.wait()
    o_buf[...] = (q_buf[...] + r_buf[...]).astype(o_buf.dtype)
    store_sum.start()
    for i in range(PIECES):
        store(i).wait()
    store_sum.wait()


def device_product(block, a_rows, b_rows):
    rows, _ = a_rows.shape
    depth, n_cols = b_rows.shape
    n_blocks, tile, unit = n_cols // block, rows // TILES, rows // sum(PARTS)
    last = n_blocks - 1
    anywhere = pl.BlockSpec(memory_space=pl.ANY)
    dma = pltpu.SemaphoreType.DMA
    parts = [jax.ShapeDtypeStruct((n * unit, block), jnp.float32) for n in PARTS]
    c_main, r_got, q_done, _, _, *split = pl.pallas_call(
        functools.partial(kernel, n_blocks, tile),
        out_shape=(
            jax.ShapeDtypeStruct((rows, n_cols), jnp.bfloat16),
            jax.ShapeDtypeStruct((last, rows, block), jnp.float32),
            jax.ShapeDtypeStruct((rows, block), jnp.float32),
            jax.ShapeDtypeStruct((3, n_blocks, depth, block), jnp.bfloat16),
            jax.ShapeDtypeStruct((2, SLAB[0], SLAB[1] * block // 4), jnp.float32),
            *parts,
            *parts,
        ),
        in_specs=[anywhere] * 2,
        out_specs=(anywhere,) * (5 + 2 * len(PARTS)),
        scratch_shapes=[
            pltpu.VMEM((2, rows, 4 * depth), jnp.bfloat16),
            pltpu.VMEM((2, 4 * depth, block), jnp.bfloat16),
            pltpu.VMEM((SLOTS, rows, block), jnp.float32),
            pltpu.VMEM((rows, block), jnp.float32),
            pltpu.VMEM((rows, block), jnp.float32),
            pltpu.VMEM((rows, block), jnp.bfloat16),
            dma((2,)),
            dma((TILES, 2)),
            dma((TILES, 2)),
            dma((3, RING)),
            dma((3, RING)),
            dma((2, 4)),
            dma((TILES,)),
            dma((TILES,)),
            dma((SLOTS,)),
            dma((RING,)),
            dma,
            dma,
            dma((len(PARTS),)),
            dma((len(PARTS),)),
            pltpu.SemaphoreType.REGULAR,
            dma((4,)),
            dma((4,)),
        ],
        compiler_params=pltpu.CompilerParams(
            collective_id=0, has_side_effects=True, vmem_limit_bytes=66_000_000
        ),
        name="split_sum_product",
    )(a_rows, b_rows)

    p_parts, q_parts = split[: len(PARTS)], split[len(PARTS) :]
    got = []
    for part in p_parts:
        got.append(lax.ppermute(part, "row", [(0, 1), (1, 0)]))
    out = pl.pallas_call(
        write_out,
        out_shape=jax.ShapeDtypeStruct((rows, n_cols), jnp.bfloat16),
        in_specs=[anywhere] * 3,
        out_specs=anywhere,
        scratch_shapes=[
            pltpu.VMEM((rows, (last - 1) * block), jnp.bfloat16),
            pltpu.VMEM((rows, block), jnp.float32),
            pltpu.VMEM((rows, block), jnp.float32),
            pltpu.VMEM((rows, block), jnp.bfloat16),
            dma((PIECES + 2,)),
            dma((PIECES + 1,)),
        ],
        compiler_params=pltpu.CompilerParams(vmem_limit_bytes=50_000_000),
        cost_estimate=pl.CostEstimate(flops=20_000_000_000, bytes_accessed=4 * rows * n_cols, transcendentals=0),
        name="write_out",
    )(c_main, q_done, r_got)
    for i, (own, part) in enumerate(zip(q_parts, got)):
        start = sum(PARTS[:i]) * unit
        out = lax.dynamic_update_slice(out, (own + part).astype(out.dtype), (start, last * block))
    return out


def solution(mesh, block=BLOCK):
    all_axes = ("depth", "row", "col")
    return jax.shard_map(
        functools.partial(device_product, block),
        mesh=mesh,
        in_specs=(P(all_axes, None), P(all_axes, None)),
        out_specs=P(all_axes, None),
        check_vma=False,
    )
```

profile of v0, /device:TPU:0, one launch (start us, length us, event | category | flops | bytes accessed | tf_op | source)
XLA Modules:
  0.0 1257.2 jit_solution(6114925576836880239)
XLA Ops:
  0.0 1210.2 %split_sum_product.1 = (bf16[1024,10240]{1,0:T(8,128)(2,1)}, f32[19,1024,512]{2,1,0:T(8,128)}, f32[1024,512]{1,0:T(8,128)}, bf16[3,20,2048,512]{3,2,1,0:T(8,128)...) custom-call(bf16[1024,16384]{1,0:T(8,128)(2,1)} %a_ref.1, ...), custom_call_target="tpu_custom_call" | custom-call | tf_op jit(solution)/shard_map/split_sum_product/pallas_call | solution.py:421
  1210.2 2.0 collective-permute-start.2
  1212.2 0.0 collective-permute-start.1
  1212.3 2.0 collective-permute-start
  1214.3 0.0 copy-start
  1214.3 1.6 copy-done
  1215.9 0.0 copy-start.1
  1215.9 0.0 copy-start.2
  1215.9 0.0 copy-start.3
  1215.9 14.5 %write_out.1 = bf16[1024,10240]{1,0:T(8,128)(2,1)} custom-call(bf16[1024,10240]{1,0:T(8,128)(2,1)} %get-tuple-element.14.c_ref, f32[1024,512]{1,0:T(8,128)S(1)} %copy-done, f32[19,1024,512]{2,1,0:T(8,128)} %get-tuple-element.16.r_ref), custom_call_target="tpu_custom_call" | custom-call | flops 20000000000 | bytes 41943040 | tf_op jit(solution)/shard_map/write_out/pallas_call | solution.py:469
  1230.4 24.3 %collective-permute-done = f32[896,512]{1,0:T(8,128)S(1)} collective-permute-done((f32[896,512]{1,0:T(8,128)}, f32[896,512]{1,0:T(8,128)S(1)}, u32[]{:S(2)}, u32[]{:S(2)}) %collective-permute-start) | collective-permute-done | bytes 1835040 | tf_op jit(solution)/shard_map/ppermute | solution.py:468
  1254.7 0.0 copy-done.1
  1254.7 1.2 fusion
  1255.9 0.0 collective-permute-done.1
  1255.9 0.0 copy-done.2
  1255.9 0.7 fusion.1
  1256.6 0.0 collective-permute-done.2
  1256.6 0.0 copy-done.3
  1256.6 0.6 fusion.2
Async XLA Ops:
  1210.2 46.4 %collective-permute-start.2 = (f32[32,512]{1,0:T(8,128)}, f32[32,512]{1,0:T(8,128)S(1)}, u32[]{:S(2)}, u32[]{:S(2)}) collective-permute-start(f32[32,512]{1,0:T(8,128)} %get-tuple-element.22), channel_id=1, source_target_pairs={{0,2},{2,0},{1,3},{3,1},{4,6},{6,4},{5,7},{7,5}} | collective-permute-start | bytes 196616 | tf_op jit(solution)/shard_map/ppermute | solution.py:468
  1212.2 43.7 %collective-permute-start.1 = (f32[96,512]{1,0:T(8,128)}, f32[96,512]{1,0:T(8,128)S(1)}, u32[]{:S(2)}, u32[]{:S(2)}) collective-permute-start(f32[96,512]{1,0:T(8,128)} %get-tuple-element.20), channel_id=1, source_target_pairs={{0,2},{2,0},{1,3},{3,1},{4,6},{6,4},{5,7},{7,5}} | collective-permute-start | bytes 589832 | tf_op jit(solution)/shard_map/ppermute | solution.py:468
  1212.3 42.4 %collective-permute-start = (f32[896,512]{1,0:T(8,128)}, f32[896,512]{1,0:T(8,128)S(1)}, u32[]{:S(2)}, u32[]{:S(2)}) collective-permute-start(f32[896,512]{1,0:T(8,128)} %get-tuple-element.18), channel_id=1, source_target_pairs={{0,2},{2,0},{1,3},{3,1},{4,6},{6,4},{5,7},{7,5}} | collective-permute-start | bytes 5505032 | tf_op jit(solution)/shard_map/ppermute | solution.py:468
  1214.3 1.6 copy-start
  1215.9 38.8 %copy-start.1 = (f32[896,512]{1,0:T(8,128)S(1)}, f32[896,512]{1,0:T(8,128)}, u32[]{:S(2)}) copy-start(f32[896,512]{1,0:T(8,128)} %get-tuple-element.17) | copy-start | bytes 5505028
  1215.9 40.1 %copy-start.2 = (f32[96,512]{1,0:T(8,128)S(1)}, f32[96,512]{1,0:T(8,128)}, u32[]{:S(2)}) copy-start(f32[96,512]{1,0:T(8,128)} %get-tuple-element.19) | copy-start | bytes 589828
  1215.9 40.7 %copy-start.3 = (f32[32,512]{1,0:T(8,128)S(1)}, f32[32,512]{1,0:T(8,128)}, u32[]{:S(2)}) copy-start(f32[32,512]{1,0:T(8,128)} %get-tuple-element.21) | copy-start | bytes 196612
where the time goes:
time: 1260 us
  Pallas kernels  1220 us (97%)
  waiting for transfers between devices  24.3 us (2%)
    pallas_call x1, Pallas kernels, device_product(): pl.pallas_call(functools.partial(kernel, n_blocks, tile), out_shape=(jax....  1210 us
  transfers between devices with their start and end apart: 3, of which 1 were waited for; matrix products, arithmetic and copies ran while one was open for 0% of the time, Pallas kernels for 1%

commit v1 on v0

--- a/solution.py
+++ b/solution.py
@@ -150,10 +150,10 @@
         def _():
             send_b(0, t + AHEAD).start()
 
-    def start_load_first(t):
+    def start_load_first(t, slot):
         send_b(1, t).wait_recv()
         send_b(2, t).wait_recv()
-        for copy in load_b(t, 0):
+        for copy in load_b(t, slot):
             copy.start()
 
     barrier = pltpu.get_barrier_semaphore()
@@ -195,7 +195,7 @@
         own_a(h).start()
     pass_on(0)
     pass_on(1)
-    start_load_first(0)
+    start_load_first(0, 0)
 
     @pl.loop(2, AHEAD)
     def _(t):
@@ -203,6 +203,7 @@
 
     for h in range(2):
         own_a(h).wait()
+    start_load_first(1, 1)
     for copy in load_b(0, 0):
         copy.wait()
 
@@ -210,26 +211,33 @@
     def _(s):
         @pl.when(s < n_blocks)
         def _():
-            @pl.when(s > 0)
+            @pl.when(s == SLOTS)
+            def _():
+                for m in range(TILES):
+                    send_first(m).wait_send()
+
+            slab_sent = jnp.logical_and(s == ROUND + SLOTS, at(0, 1))
+
+            @pl.when(jnp.logical_and(s > SLOTS, jnp.logical_not(slab_sent)))
+            def _():
+                send_block(s - SLOTS).wait_send()
+
+            @pl.when(slab_sent)
+            def _():
+                for copy in (*send_rest(), hop(0)):
+                    copy.wait_send()
+
+            @pl.when(s == 1)
+            def _():
+                for copy in load_b(1, 1):
+                    copy.wait()
+
+            @pl.when(s > 1)
             def _():
                 for copy in load_b(s, 0):
                     copy.wait()
 
-            @pl.when(s == SLOTS)
-            def _():
-                for m in range(TILES):
-                    send_first(m).wait_send()
-
-            slab_sent = jnp.logical_and(s == ROUND + SLOTS, at(0, 1))
-
-            @pl.when(jnp.logical_and(s > SLOTS, jnp.logical_not(slab_sent)))
-            def _():
-                send_block(s - SLOTS).wait_send()
-
-            @pl.when(slab_sent)
-            def _():
-                for copy in (*send_rest(), hop(0)):
-                    copy.wait_send()
+            slot = jnp.where(s == 1, 1, 0)
 
             @pl.loop(0, TILES)
             def _(m):
@@ -238,7 +246,7 @@
                     for h in range(2):
                         send_a(m, h).wait_recv()
 
-                p_buf[lax.rem(s, SLOTS), rows_of(m), :] = product(1, m, 0)
+                p_buf[lax.rem(s, SLOTS), rows_of(m), :] = product(1, m, slot)
 
                 held = jnp.logical_and(core == 1, m < len(early))
 
@@ -278,9 +286,13 @@
             def _():
                 pass_on(s + AHEAD)
 
-            @pl.when(s + 1 < n_blocks)
-            def _():
-                start_load_first(s + 1)
+            @pl.when(s == 0)
+            def _():
+                start_load_first(2, 0)
+
+            @pl.when(jnp.logical_and(s > 1, s + 1 < n_blocks))
+            def _():
+                start_load_first(s + 1, 0)
 
         @pl.when(s >= SLOTS)
         def _():

time: 1260 us -> 1260 us (level)
  no operation moved by 1% of the time
where the time goes in v1:
time: 1260 us
  Pallas kernels  1220 us (97%)
  waiting for transfers between devices  24.3 us (2%)
    pallas_call x1, Pallas kernels, device_product(): pl.pallas_call(functools.partial(kernel, n_blocks, tile), out_shape=(jax....  1210 us
  transfers between devices with their start and end apart: 3, of which 1 were waited for; matrix products, arithmetic and copies ran while one was open for 0% of the time, Pallas kernels for 1%

profile of v1, /device:TPU:0, one launch (start us, length us, event | category | flops | bytes accessed | tf_op | source)
XLA Modules:
  0.0 1257.2 jit_solution(12700532342184661841)
XLA Ops:
  0.0 1210.2 %split_sum_product.1 = (bf16[1024,10240]{1,0:T(8,128)(2,1)}, f32[19,1024,512]{2,1,0:T(8,128)}, f32[1024,512]{1,0:T(8,128)}, bf16[3,20,2048,512]{3,2,1,0:T(8,128)...) custom-call(bf16[1024,16384]{1,0:T(8,128)(2,1)} %a_ref.1, ...), custom_call_target="tpu_custom_call" | custom-call | tf_op jit(solution)/shard_map/split_sum_product/pallas_call | solution.py:433
  1210.2 2.0 collective-permute-start.2
  1212.2 0.0 collective-permute-start.1
  1212.2 2.0 collective-permute-start
  1214.2 0.0 copy-start
  1214.2 1.6 copy-done
  1215.8 0.0 copy-start.1
  1215.8 0.0 copy-start.2
  1215.8 0.0 copy-start.3
  1215.8 14.5 %write_out.1 = bf16[1024,10240]{1,0:T(8,128)(2,1)} custom-call(bf16[1024,10240]{1,0:T(8,128)(2,1)} %get-tuple-element.14.c_ref, f32[1024,512]{1,0:T(8,128)S(1)} %copy-done, f32[19,1024,512]{2,1,0:T(8,128)} %get-tuple-element.16.r_ref), custom_call_target="tpu_custom_call" | custom-call | flops 20000000000 | bytes 41943040 | tf_op jit(solution)/shard_map/write_out/pallas_call | solution.py:481
  1230.3 24.3 %collective-permute-done = f32[896,512]{1,0:T(8,128)S(1)} collective-permute-done((f32[896,512]{1,0:T(8,128)}, f32[896,512]{1,0:T(8,128)S(1)}, u32[]{:S(2)}, u32[]{:S(2)}) %collective-permute-start) | collective-permute-done | bytes 1835040 | tf_op jit(solution)/shard_map/ppermute | solution.py:480
  1254.7 0.0 copy-done.1
  1254.7 1.2 fusion
  1255.9 0.0 collective-permute-done.1
  1255.9 0.0 copy-done.2
  1255.9 0.7 fusion.1
  1256.6 0.0 collective-permute-done.2
  1256.6 0.0 copy-done.3
  1256.6 0.6 fusion.2
Async XLA Ops:
  1210.2 46.4 %collective-permute-start.2 = (f32[32,512]{1,0:T(8,128)}, f32[32,512]{1,0:T(8,128)S(1)}, u32[]{:S(2)}, u32[]{:S(2)}) collective-permute-start(f32[32,512]{1,0:T(8,128)} %get-tuple-element.22), channel_id=1, source_target_pairs={{0,2},{2,0},{1,3},{3,1},{4,6},{6,4},{5,7},{7,5}} | collective-permute-start | bytes 196616 | tf_op jit(solution)/shard_map/ppermute | solution.py:480
  1212.2 43.7 %collective-permute-start.1 = (f32[96,512]{1,0:T(8,128)}, f32[96,512]{1,0:T(8,128)S(1)}, u32[]{:S(2)}, u32[]{:S(2)}) collective-permute-start(f32[96,512]{1,0:T(8,128)} %get-tuple-element.20), channel_id=1, source_target_pairs={{0,2},{2,0},{1,3},{3,1},{4,6},{6,4},{5,7},{7,5}} | collective-permute-start | bytes 589832 | tf_op jit(solution)/shard_map/ppermute | solution.py:480
  1212.2 42.4 %collective-permute-start = (f32[896,512]{1,0:T(8,128)}, f32[896,512]{1,0:T(8,128)S(1)}, u32[]{:S(2)}, u32[]{:S(2)}) collective-permute-start(f32[896,512]{1,0:T(8,128)} %get-tuple-element.18), channel_id=1, source_target_pairs={{0,2},{2,0},{1,3},{3,1},{4,6},{6,4},{5,7},{7,5}} | collective-permute-start | bytes 5505032 | tf_op jit(solution)/shard_map/ppermute | solution.py:480
  1214.2 1.6 copy-start
  1215.8 38.8 %copy-start.1 = (f32[896,512]{1,0:T(8,128)S(1)}, f32[896,512]{1,0:T(8,128)}, u32[]{:S(2)}) copy-start(f32[896,512]{1,0:T(8,128)} %get-tuple-element.17) | copy-start | bytes 5505028
  1215.8 40.1 %copy-start.2 = (f32[96,512]{1,0:T(8,128)S(1)}, f32[96,512]{1,0:T(8,128)}, u32[]{:S(2)}) copy-start(f32[96,512]{1,0:T(8,128)} %get-tuple-element.19) | copy-start | bytes 589828
  1215.8 40.7 %copy-start.3 = (f32[32,512]{1,0:T(8,128)S(1)}, f32[32,512]{1,0:T(8,128)}, u32[]{:S(2)}) copy-start(f32[32,512]{1,0:T(8,128)} %get-tuple-element.21) | copy-start | bytes 196612

commit v2 on v0

--- a/solution.py
+++ b/solution.py
@@ -13,7 +13,7 @@
 TILES = 4
 AHEAD = 4
 SLOTS = 3
-PARTS = (28, 3, 1)
+PARTS = (1, 20, 20, 15, 6, 2)
 HUB = (1, 0)
 SLAB = (16, 3)
 ROUND = 8
@@ -21,10 +21,18 @@
 RING = 2 * (SLOTS + 1)
 
 
+def rectangles(rows, columns):
+    unit, half = rows // sum(PARTS), columns // 2
+    starts = [sum(PARTS[:i]) * unit for i in range(len(PARTS))]
+    whole = [(start, 0, n * unit, columns) for start, n in zip(starts, PARTS)]
+    return [(0, 0, PARTS[0] * unit, half), (0, half, PARTS[0] * unit, half), *whole[1:]]
+
+
 def kernel(
     n_blocks, tile, a_ref, b_ref, c_ref, r_got, q_done, b_got, relay, *others,
 ):
-    p_parts, q_parts, scratch = others[: len(PARTS)], others[len(PARTS) : 2 * len(PARTS)], others[2 * len(PARTS) :]
+    n_parts = len(PARTS) + 1
+    p_parts, q_parts, scratch = others[:n_parts], others[n_parts : 2 * n_parts], others[2 * n_parts :]
     (
         a_buf, b_buf, p_buf, q_buf, r_buf, c_buf,
         a_own_sem, a_send, a_recv, b_send, b_recv, b_load_sem, first_send, first_recv, p_send, r_recv,
@@ -111,21 +119,23 @@
     def store_c(q):
         return pltpu.make_async_copy(c_buf, c_ref.at[:, cols_of(q)], c_sem)
 
-    unit = p_buf.shape[1] // sum(PARTS)
-    parts = [pl.ds(sum(PARTS[:i]) * unit, n * unit) for i, n in enumerate(PARTS)]
+    parts = [
+        (pl.ds(row_, rows_), pl.ds(column, columns))
+        for row_, column, rows_, columns in rectangles(p_buf.shape[1], block)
+    ]
 
     def store_q_done():
         return pltpu.make_async_copy(q_buf, q_done, q_sem.at[0])
 
     def store_q():
         return [
-            pltpu.make_async_copy(q_buf.at[part], out, q_sem.at[i])
+            pltpu.make_async_copy(q_buf.at[*part], out, q_sem.at[i])
             for i, (part, out) in enumerate(zip(parts, q_parts))
         ]
 
     def store_p():
         return [
-            pltpu.make_async_copy(p_buf.at[last % SLOTS, part], out, last_sem.at[i])
+            pltpu.make_async_copy(p_buf.at[last % SLOTS, *part], out, last_sem.at[i])
             for i, (part, out) in enumerate(zip(parts, p_parts))
         ]
 
@@ -413,11 +423,11 @@
 def device_product(block, a_rows, b_rows):
     rows, _ = a_rows.shape
     depth, n_cols = b_rows.shape
-    n_blocks, tile, unit = n_cols // block, rows // TILES, rows // sum(PARTS)
+    n_blocks, tile, n_parts = n_cols // block, rows // TILES, len(PARTS) + 1
     last = n_blocks - 1
     anywhere = pl.BlockSpec(memory_space=pl.ANY)
     dma = pltpu.SemaphoreType.DMA
-    parts = [jax.ShapeDtypeStruct((n * unit, block), jnp.float32) for n in PARTS]
+    parts = [jax.ShapeDtypeStruct(place[2:], jnp.float32) for place in rectangles(rows, block)]
     c_main, r_got, q_done, _, _, *split = pl.pallas_call(
         functools.partial(kernel, n_blocks, tile),
         out_shape=(
@@ -430,7 +440,7 @@
             *parts,
         ),
         in_specs=[anywhere] * 2,
-        out_specs=(anywhere,) * (5 + 2 * len(PARTS)),
+        out_specs=(anywhere,) * (5 + 2 * n_parts),
         scratch_shapes=[
             pltpu.VMEM((2, rows, 4 * depth), jnp.bfloat16),
             pltpu.VMEM((2, 4 * depth, block), jnp.bfloat16),
@@ -450,8 +460,8 @@
             dma((RING,)),
             dma,
             dma,
-            dma((len(PARTS),)),
-            dma((len(PARTS),)),
+            dma((n_parts,)),
+            dma((n_parts,)),
             pltpu.SemaphoreType.REGULAR,
             dma((4,)),
             dma((4,)),
@@ -462,10 +472,14 @@
         name="split_sum_product",
     )(a_rows, b_rows)
 
-    p_parts, q_parts = split[: len(PARTS)], split[len(PARTS) :]
+    p_parts, q_parts = split[:n_parts], split[n_parts:]
+    pair = ("row", "depth")
     got = []
-    for part in p_parts:
-        got.append(lax.ppermute(part, "row", [(0, 1), (1, 0)]))
+    lent = lax.ppermute(q_parts[0], pair, [(1, 3)])
+    got.append(lax.ppermute(p_parts[0], pair, [(0, 2), (1, 3), (2, 0)]))
+    for i, part in enumerate(p_parts[1:], 1):
+        got.append(lax.ppermute(part, pair, [(0, 2), (1, 3), (2, 0), (3, 1)]))
+    back = lax.ppermute((lent + p_parts[0]).astype(jnp.bfloat16), pair, [(3, 1)])
     out = pl.pallas_call(
         write_out,
         out_shape=jax.ShapeDtypeStruct((rows, n_cols), jnp.bfloat16),
@@ -483,9 +497,12 @@
         cost_estimate=pl.CostEstimate(flops=20_000_000_000, bytes_accessed=4 * rows * n_cols, transcendentals=0),
         name="write_out",
     )(c_main, q_done, r_got)
-    for i, (own, part) in enumerate(zip(q_parts, got)):
-        start = sum(PARTS[:i]) * unit
-        out = lax.dynamic_update_slice(out, (own + part).astype(out.dtype), (start, last * block))
+    finished = [(own + part).astype(out.dtype) for own, part in zip(q_parts, got)]
+    lender = jnp.logical_and(lax.axis_index("row") == 0, lax.axis_index("depth") == 1)
+    finished[0] = jnp.where(lender, back, finished[0])
+    places = rectangles(rows, block)
+    for i in (2, 1, 3, 0, *range(4, n_parts)):
+        out = lax.dynamic_update_slice(out, finished[i], (places[i][0], last * block + places[i][1]))
     return out
 
 

time: 1260 us -> 1270 us (level)
  transfers between devices with their start and end apart: 3 -> 9, of which waited for: 1 -> 2; matrix products, arithmetic and copies ran while one was open for 0% -> 0% of each run, Pallas kernels for 1% -> 1%
where the time goes in v2:
time: 1270 us; the launch traced here: 1250 us
  Pallas kernels  1220 us (96%)
    pallas_call x1, Pallas kernels, device_product(): pl.pallas_call(functools.partial(kernel, n_blocks, tile), out_shape=(jax....  1210 us
  transfers between devices with their start and end apart: 9, of which 2 were waited for; matrix products, arithmetic and copies ran while one was open for 0% of the time, Pallas kernels for 1%

profile of v2, /device:TPU:0, one launch (start us, length us, event | category | flops | bytes accessed | tf_op | source)
XLA Modules:
  0.0 1254.7 jit_solution(12637203804195317607)
XLA Ops:
  0.0 1210.3 %split_sum_product.1 = (bf16[1024,10240]{1,0:T(8,128)(2,1)}, f32[19,1024,512]{2,1,0:T(8,128)}, f32[1024,512]{1,0:T(8,128)}, bf16[3,20,2048,512]{3,2,1,0:T(8,128)...) custom-call(bf16[1024,16384]{1,0:T(8,128)(2,1)} %a_ref.1, ...), custom_call_target="tpu_custom_call" | custom-call | tf_op jit(solution)/shard_map/split_sum_product/pallas_call | solution.py:431
  1210.3 2.0 collective-permute-start
  1212.3 0.0 collective-permute-start.1
  1212.4 2.0 collective-permute-start.2
  1214.3 0.7 collective-permute-start.3
  1215.0 1.9 collective-permute-start.5
  1217.0 1.6 copy-done
  1218.6 14.5 %write_out.1 = bf16[1024,10240]{1,0:T(8,128)(2,1)} custom-call(bf16[1024,10240]{1,0:T(8,128)(2,1)} %get-tuple-element.22.c_ref, f32[1024,512]{1,0:T(8,128)S(1)} %copy-done, f32[19,1024,512]{2,1,0:T(8,128)} %get-tuple-element.24.r_ref), custom_call_target="tpu_custom_call" | custom-call | flops 20000000000 | bytes 41943040 | tf_op jit(solution)/shard_map/write_out/pallas_call | solution.py:483
  1233.1 2.0 collective-permute-start.6
  1235.1 0.0 collective-permute-done
  1235.1 0.1 collective-permute-start.7
  1235.2 0.8 fusion
  1236.0 0.0 collective-permute-done.1
  1236.0 2.0 collective-permute-start.8
  1238.0 0.6 fusion.5
  1238.6 0.7 collective-permute-start.4
  1239.3 0.8 fusion.1
  1240.1 0.6 fusion.7
  1240.7 8.4 collective-permute-done.6
  1249.1 0.8 fusion.2
  1249.9 3.4 collective-permute-done.7
  1253.4 0.7 fusion.3
  1254.0 0.0 collective-permute-done.8
  1254.1 0.6 fusion.4
  (24 shorter events, 0.1 us)
Async XLA Ops:
  1210.3 24.8 %collective-permute-start = (f32[320,512]{1,0:T(8,128)}, f32[320,512]{1,0:T(8,128)S(1)}, u32[]{:S(2)}, u32[]{:S(2)}) collective-permute-start(f32[320,512]{1,0:T(8,128)} %get-tuple-element.26), channel_id=1, source_target_pairs={{0,2},{1,3},{2,0},{3,1},{4,6},{5,7},{6,4},{7,5}} | collective-permute-start | bytes 1966088 | tf_op jit(solution)/shard_map/ppermute | solution.py:481
  1212.3 23.7 %collective-permute-start.1 = (f32[16,256]{1,0:T(8,128)}, f32[16,256]{1,0:T(8,128)S(1)}, u32[]{:S(2)}, u32[]{:S(2)}) collective-permute-start(f32[16,256]{1,0:T(8,128)} %get-tuple-element.28), channel_id=1, source_target_pairs={{0,2},{1,3},{2,0},{3,1},{4,6},{5,7},{6,4},{7,5}} | collective-permute-start | bytes 49160 | tf_op jit(solution)/shard_map/ppermute | solution.py:481
  1212.4 26.3 %collective-permute-start.2 = (f32[320,512]{1,0:T(8,128)}, f32[320,512]{1,0:T(8,128)S(1)}, u32[]{:S(2)}, u32[]{:S(2)}) collective-permute-start(f32[320,512]{1,0:T(8,128)} %get-tuple-element.30), channel_id=1, source_target_pairs={{0,2},{1,3},{2,0},{3,1},{4,6},{5,7},{6,4},{7,5}} | collective-permute-start | bytes 1966088 | tf_op jit(solution)/shard_map/ppermute | solution.py:481
  1214.3 18.8 %collective-permute-start.3 = (f32[16,256]{1,0:T(8,128)}, f32[16,256]{1,0:T(8,128)S(1)}, u32[]{:S(2)}, u32[]{:S(2)}) collective-permute-start(f32[16,256]{1,0:T(8,128)} %get-tuple-element.31), channel_id=1, source_target_pairs={{1,3},{5,7}} | collective-permute-start | bytes 49160 | tf_op jit(solution)/shard_map/ppermute | solution.py:478
  1215.0 25.1 %collective-permute-start.5 = (f32[16,256]{1,0:T(8,128)}, f32[16,256]{1,0:T(8,128)S(1)}, u32[]{:S(2)}, u32[]{:S(2)}) collective-permute-start(f32[16,256]{1,0:T(8,128)} %get-tuple-element.32), channel_id=1, source_target_pairs={{0,2},{1,3},{2,0},{4,6},{5,7},{6,4}} | collective-permute-start | bytes 49160 | tf_op jit(solution)/shard_map/ppermute | solution.py:479
  1217.0 1.6 copy-start
  1218.5 16.6 %copy-start.7 = (f32[16,256]{1,0:T(8,128)S(1)}, f32[16,256]{1,0:T(8,128)}, u32[]{:S(2)}) copy-start(f32[16,256]{1,0:T(8,128)} %get-tuple-element.32) | copy-start | bytes 49156
  1218.5 16.7 %copy-start.2 = (f32[320,512]{1,0:T(8,128)S(1)}, f32[320,512]{1,0:T(8,128)}, u32[]{:S(2)}) copy-start(f32[320,512]{1,0:T(8,128)} %get-tuple-element.25) | copy-start | bytes 1966084
  1218.5 17.5 %copy-start.9 = (f32[32,512]{1,0:T(8,128)S(1)}, f32[32,512]{1,0:T(8,128)}, u32[]{:S(2)}) copy-start(f32[32,512]{1,0:T(8,128)} %get-tuple-element.38) | copy-start | bytes 196612
  1218.6 19.5 %copy-start.8 = (f32[16,256]{1,0:T(8,128)S(1)}, f32[16,256]{1,0:T(8,128)}, u32[]{:S(2)}) copy-start(f32[16,256]{1,0:T(8,128)} %get-tuple-element.27) | copy-start | bytes 49156
  1218.6 20.7 %copy-start.1 = (f32[320,512]{1,0:T(8,128)S(1)}, f32[320,512]{1,0:T(8,128)}, u32[]{:S(2)}) copy-start(f32[320,512]{1,0:T(8,128)} %get-tuple-element.29) | copy-start | bytes 1966084
  1218.6 21.5 %copy-start.6 = (f32[16,256]{1,0:T(8,128)S(1)}, f32[16,256]{1,0:T(8,128)}, u32[]{:S(2)}) copy-start(f32[16,256]{1,0:T(8,128)} %get-tuple-element.31) | copy-start | bytes 49156
  1218.6 30.6 %copy-start.3 = (f32[240,512]{1,0:T(8,128)S(1)}, f32[240,512]{1,0:T(8,128)}, u32[]{:S(2)}) copy-start(f32[240,512]{1,0:T(8,128)} %get-tuple-element.33) | copy-start | bytes 1474564
  1218.6 34.8 %copy-start.4 = (f32[96,512]{1,0:T(8,128)S(1)}, f32[96,512]{1,0:T(8,128)}, u32[]{:S(2)}) copy-start(f32[96,512]{1,0:T(8,128)} %get-tuple-element.35) | copy-start | bytes 589828
  1218.6 35.5 %copy-start.5 = (f32[32,512]{1,0:T(8,128)S(1)}, f32[32,512]{1,0:T(8,128)}, u32[]{:S(2)}) copy-start(f32[32,512]{1,0:T(8,128)} %get-tuple-element.37) | copy-start | bytes 196612
  1233.1 16.0 %collective-permute-start.6 = (f32[240,512]{1,0:T(8,128)}, f32[240,512]{1,0:T(8,128)S(1)}, u32[]{:S(2)}, u32[]{:S(2)}) collective-permute-start(f32[240,512]{1,0:T(8,128)} %get-tuple-element.34), channel_id=1, source_target_pairs={{0,2},{1,3},{2,0},{3,1},{4,6},{5,7},{6,4},{7,5}} | collective-permute-start | bytes 1474568 | tf_op jit(solution)/shard_map/ppermute | solution.py:481
  1235.1 18.2 %collective-permute-start.7 = (f32[96,512]{1,0:T(8,128)}, f32[96,512]{1,0:T(8,128)S(1)}, u32[]{:S(2)}, u32[]{:S(2)}) collective-permute-start(f32[96,512]{1,0:T(8,128)} %get-tuple-element.36), channel_id=1, source_target_pairs={{0,2},{1,3},{2,0},{3,1},{4,6},{5,7},{6,4},{7,5}} | collective-permute-start | bytes 589832 | tf_op jit(solution)/shard_map/ppermute | solution.py:481
  1236.0 18.0 %collective-permute-start.8 = (f32[32,512]{1,0:T(8,128)S(1)}, f32[32,512]{1,0:T(8,128)S(1)}, u32[]{:S(2)}, u32[]{:S(2)}) collective-permute-start(f32[32,512]{1,0:T(8,128)S(1)} %copy-done.9), channel_id=1, source_target_pairs={{0,2},{1,3},{2,0},{3,1},{4,6},{5,7},{6,4},{7,5}} | collective-permute-start | bytes 196616 | tf_op jit(solution)/shard_map/ppermute | solution.py:481
  1238.6 1.5 collective-permute-start.4

commit v3 on v0

--- a/solution.py
+++ b/solution.py
@@ -17,12 +17,11 @@
 HUB = (1, 0)
 SLAB = (16, 3)
 ROUND = 8
-PIECES = 1
 RING = 2 * (SLOTS + 1)
 
 
 def kernel(
-    n_blocks, tile, a_ref, b_ref, c_ref, r_got, q_done, b_got, relay, *others,
+    n_blocks, tile, a_ref, b_ref, c_ref, r_got, b_got, relay, *others,
 ):
     p_parts, q_parts, scratch = others[: len(PARTS)], others[len(PARTS) : 2 * len(PARTS)], others[2 * len(PARTS) :]
     (
@@ -114,12 +113,9 @@
     unit = p_buf.shape[1] // sum(PARTS)
     parts = [pl.ds(sum(PARTS[:i]) * unit, n * unit) for i, n in enumerate(PARTS)]
 
-    def store_q_done():
-        return pltpu.make_async_copy(q_buf, q_done, q_sem.at[0])
-
     def store_q():
         return [
-            pltpu.make_async_copy(q_buf.at[part], out, q_sem.at[i])
+            pltpu.make_async_copy(q_buf.at[1, part], out, q_sem.at[i])
             for i, (part, out) in enumerate(zip(parts, q_parts))
         ]
 
@@ -155,6 +151,20 @@
         send_b(2, t).wait_recv()
         for copy in load_b(t, 0):
             copy.start()
+
+    def finish(q):
+        load_r(q).wait()
+
+        @pl.when(q > 0)
+        def _():
+            store_c(q - 1).wait()
+
+        @pl.loop(0, TILES)
+        def _(m):
+            rows = rows_of(m)
+            c_buf[rows, :] = (q_buf[0, rows, :] + r_buf[rows, :]).astype(c_buf.dtype)
+
+        store_c(q).start()
 
     barrier = pltpu.get_barrier_semaphore()
     is_hub = jnp.logical_and(col == HUB[0], core == HUB[1])
@@ -309,17 +319,11 @@
             for copy in load_b(q, 1):
                 copy.wait()
 
-            @pl.when(q == last)
-            def _():
-                store_q_done().wait()
+            mine = jnp.where(q == last, 1, 0)
 
             @pl.loop(0, TILES)
             def _(m):
-                q_buf[rows_of(m), :] = product(0, m, 1)
-
-            @pl.when(q == last - 1)
-            def _():
-                store_q_done().start()
+                q_buf[mine, rows_of(m), :] = product(0, m, 1)
 
             @pl.when(q == last)
             def _():
@@ -333,18 +337,7 @@
 
             @pl.when(q < last - 1)
             def _():
-                load_r(q).wait()
-
-                @pl.when(q > 0)
-                def _():
-                    store_c(q - 1).wait()
-
-                @pl.loop(0, TILES)
-                def _(m):
-                    rows = rows_of(m)
-                    c_buf[rows, :] = (q_buf[rows, :] + r_buf[rows, :]).astype(c_buf.dtype)
-
-                store_c(q).start()
+                finish(q)
 
         @pl.when(s == SLOTS - 1)
         def _():
@@ -365,7 +358,6 @@
         def _():
             hop(i).wait_send()
 
-    store_c(last - 2).wait()
     for copy in store_q() + store_p():
         copy.wait()
     for m in range(TILES):
@@ -377,37 +369,19 @@
         send_block(s).wait_send()
 
     send_block(last - 1).wait_recv()
-
-
-def write_out(c_ref, q_ref, r_ref, out_ref, c_buf, q_buf, r_buf, o_buf, load_sem, store_sem):
-    rows, done = c_buf.shape
-    step = rows // PIECES
-
-    def load(i):
-        some = pl.ds(i * step, step)
-        return pltpu.make_async_copy(c_ref.at[some, pl.ds(0, done)], c_buf.at[some], load_sem.at[i])
-
-    def store(i):
-        some = pl.ds(i * step, step)
-        return pltpu.make_async_copy(c_buf.at[some], out_ref.at[some, pl.ds(0, done)], store_sem.at[i])
-
-    load_q = pltpu.make_async_copy(q_ref, q_buf, load_sem.at[PIECES])
-    load_r = pltpu.make_async_copy(r_ref.at[r_ref.shape[0] - 1], r_buf, load_sem.at[PIECES + 1])
-    store_sum = pltpu.make_async_copy(o_buf, out_ref.at[:, pl.ds(done, o_buf.shape[1])], store_sem.at[PIECES])
-    load_q.start()
-    load_r.start()
-    for i in range(PIECES):
-        load(i).start()
-    for i in range(PIECES):
-        load(i).wait()
-        store(i).start()
-    load_q.wait()
-    load_r.wait()
-    o_buf[...] = (q_buf[...] + r_buf[...]).astype(o_buf.dtype)
-    store_sum.start()
-    for i in range(PIECES):
-        store(i).wait()
-    store_sum.wait()
+    load_r(last - 1).start()
+    finish(last - 1)
+    store_c(last - 1).wait()
+
+
+def write_out(c_ref, out_ref, c_buf, load_sem, store_sem):
+    done = pl.ds(0, c_buf.shape[1])
+    load = pltpu.make_async_copy(c_ref.at[:, done], c_buf, load_sem)
+    store = pltpu.make_async_copy(c_buf, out_ref.at[:, done], store_sem)
+    load.start()
+    load.wait()
+    store.start()
+    store.wait()
 
 
 def device_product(block, a_rows, b_rows):
@@ -418,24 +392,23 @@
     anywhere = pl.BlockSpec(memory_space=pl.ANY)
     dma = pltpu.SemaphoreType.DMA
     parts = [jax.ShapeDtypeStruct((n * unit, block), jnp.float32) for n in PARTS]
-    c_main, r_got, q_done, _, _, *split = pl.pallas_call(
+    c_main, _, _, _, *split = pl.pallas_call(
         functools.partial(kernel, n_blocks, tile),
         out_shape=(
             jax.ShapeDtypeStruct((rows, n_cols), jnp.bfloat16),
             jax.ShapeDtypeStruct((last, rows, block), jnp.float32),
-            jax.ShapeDtypeStruct((rows, block), jnp.float32),
             jax.ShapeDtypeStruct((3, n_blocks, depth, block), jnp.bfloat16),
             jax.ShapeDtypeStruct((2, SLAB[0], SLAB[1] * block // 4), jnp.float32),
             *parts,
             *parts,
         ),
         in_specs=[anywhere] * 2,
-        out_specs=(anywhere,) * (5 + 2 * len(PARTS)),
+        out_specs=(anywhere,) * (4 + 2 * len(PARTS)),
         scratch_shapes=[
             pltpu.VMEM((2, rows, 4 * depth), jnp.bfloat16),
             pltpu.VMEM((2, 4 * depth, block), jnp.bfloat16),
             pltpu.VMEM((SLOTS, rows, block), jnp.float32),
-            pltpu.VMEM((rows, block), jnp.float32),
+            pltpu.VMEM((2, rows, block), jnp.float32),
             pltpu.VMEM((rows, block), jnp.float32),
             pltpu.VMEM((rows, block), jnp.bfloat16),
             dma((2,)),
@@ -469,20 +442,13 @@
     out = pl.pallas_call(
         write_out,
         out_shape=jax.ShapeDtypeStruct((rows, n_cols), jnp.bfloat16),
-        in_specs=[anywhere] * 3,
+        in_specs=[anywhere],
         out_specs=anywhere,
-        scratch_shapes=[
-            pltpu.VMEM((rows, (last - 1) * block), jnp.bfloat16),
-            pltpu.VMEM((rows, block), jnp.float32),
-            pltpu.VMEM((rows, block), jnp.float32),
-            pltpu.VMEM((rows, block), jnp.bfloat16),
-            dma((PIECES + 2,)),
-            dma((PIECES + 1,)),
-        ],
+        scratch_shapes=[pltpu.VMEM((rows, last * block), jnp.bfloat16), dma, dma],
         compiler_params=pltpu.CompilerParams(vmem_limit_bytes=50_000_000),
         cost_estimate=pl.CostEstimate(flops=20_000_000_000, bytes_accessed=4 * rows * n_cols, transcendentals=0),
         name="write_out",
-    )(c_main, q_done, r_got)
+    )(c_main)
     for i, (own, part) in enumerate(zip(q_parts, got)):
         start = sum(PARTS[:i]) * unit
         out = lax.dynamic_update_slice(out, (own + part).astype(out.dtype), (start, last * block))

time: 1260 us -> 1260 us (level)
  no operation moved by 1% of the time
where the time goes in v3:
time: 1260 us
  Pallas kernels  1230 us (98%)
  waiting for transfers between devices  25.2 us (2%)
    pallas_call x1, Pallas kernels, device_product(): pl.pallas_call(functools.partial(kernel, n_blocks, tile), out_shape=(jax....  1210 us
  transfers between devices with their start and end apart: 3, of which 1 were waited for; matrix products, arithmetic and copies ran while one was open for 0% of the time, Pallas kernels for 1%

profile of v3, /device:TPU:0, one launch (start us, length us, event | category | flops | bytes accessed | tf_op | source)
XLA Modules:
  0.0 1258.8 jit_solution(496794705540220001)
XLA Ops:
  0.0 1213.1 %split_sum_product.1 = (bf16[1024,10240]{1,0:T(8,128)(2,1)}, f32[19,1024,512]{2,1,0:T(8,128)}, bf16[3,20,2048,512]{3,2,1,0:T(8,128)(2,1)}, f32[2,16,384]{2,1,0:T...) custom-call(bf16[1024,16384]{1,0:T(8,128)(2,1)} %a_ref.1, ...), custom_call_target="tpu_custom_call" | custom-call | tf_op jit(solution)/shard_map/split_sum_product/pallas_call | solution.py:395
  1213.1 2.0 collective-permute-start.2
  1215.1 0.0 collective-permute-start.1
  1215.1 2.0 collective-permute-start
  1217.1 0.0 copy-start
  1217.1 0.0 copy-start.1
  1217.1 0.0 copy-start.2
  1217.1 14.0 %write_out.1 = bf16[1024,10240]{1,0:T(8,128)(2,1)} custom-call(bf16[1024,10240]{1,0:T(8,128)(2,1)} %get-tuple-element.12.c_ref), custom_call_target="tpu_custom_call" | custom-call | flops 20000000000 | bytes 41943040 | tf_op jit(solution)/shard_map/write_out/pallas_call | solution.py:442
  1231.2 25.1 %collective-permute-done = f32[896,512]{1,0:T(8,128)S(1)} collective-permute-done((f32[896,512]{1,0:T(8,128)}, f32[896,512]{1,0:T(8,128)S(1)}, u32[]{:S(2)}, u32[]{:S(2)}) %collective-permute-start) | collective-permute-done | bytes 1835040 | tf_op jit(solution)/shard_map/ppermute | solution.py:441
  1256.3 0.0 copy-done
  1256.3 1.2 fusion
  1257.5 0.0 collective-permute-done.1
  1257.5 0.0 copy-done.1
  1257.5 0.7 fusion.1
  1258.2 0.0 collective-permute-done.2
  1258.2 0.0 copy-done.2
  1258.2 0.6 fusion.2
Async XLA Ops:
  1213.1 45.1 %collective-permute-start.2 = (f32[32,512]{1,0:T(8,128)}, f32[32,512]{1,0:T(8,128)S(1)}, u32[]{:S(2)}, u32[]{:S(2)}) collective-permute-start(f32[32,512]{1,0:T(8,128)} %get-tuple-element.18), channel_id=1, source_target_pairs={{0,2},{2,0},{1,3},{3,1},{4,6},{6,4},{5,7},{7,5}} | collective-permute-start | bytes 196616 | tf_op jit(solution)/shard_map/ppermute | solution.py:441
  1215.1 42.4 %collective-permute-start.1 = (f32[96,512]{1,0:T(8,128)}, f32[96,512]{1,0:T(8,128)S(1)}, u32[]{:S(2)}, u32[]{:S(2)}) collective-permute-start(f32[96,512]{1,0:T(8,128)} %get-tuple-element.16), channel_id=1, source_target_pairs={{0,2},{2,0},{1,3},{3,1},{4,6},{6,4},{5,7},{7,5}} | collective-permute-start | bytes 589832 | tf_op jit(solution)/shard_map/ppermute | solution.py:441
  1215.1 41.2 %collective-permute-start = (f32[896,512]{1,0:T(8,128)}, f32[896,512]{1,0:T(8,128)S(1)}, u32[]{:S(2)}, u32[]{:S(2)}) collective-permute-start(f32[896,512]{1,0:T(8,128)} %get-tuple-element.14), channel_id=1, source_target_pairs={{0,2},{2,0},{1,3},{3,1},{4,6},{6,4},{5,7},{7,5}} | collective-permute-start | bytes 5505032 | tf_op jit(solution)/shard_map/ppermute | solution.py:441
  1217.1 39.2 %copy-start = (f32[896,512]{1,0:T(8,128)S(1)}, f32[896,512]{1,0:T(8,128)}, u32[]{:S(2)}) copy-start(f32[896,512]{1,0:T(8,128)} %get-tuple-element.13) | copy-start | bytes 5505028
  1217.1 40.4 %copy-start.1 = (f32[96,512]{1,0:T(8,128)S(1)}, f32[96,512]{1,0:T(8,128)}, u32[]{:S(2)}) copy-start(f32[96,512]{1,0:T(8,128)} %get-tuple-element.15) | copy-start | bytes 589828
  1217.1 41.1 %copy-start.2 = (f32[32,512]{1,0:T(8,128)S(1)}, f32[32,512]{1,0:T(8,128)}, u32[]{:S(2)}) copy-start(f32[32,512]{1,0:T(8,128)} %get-tuple-element.17) | copy-start | bytes 196612
